TPU v7x, 32 devices: a whole 2x2x4 slice. The times are simulated.
32 devices in a mesh: dp: 2 (over x), tp: 16 (over y, z, core).
Axes of the slice: x: 2, y: 2, z: 4, core: 2. Of those that a mesh axis runs over, the one named last changes fastest.
Arguments:
- x: bfloat16 [4096, 4096], P('dp'), parts along dimension 0
- dy: bfloat16 [4096, 4096], P('dp'), parts along dimension 0
- gate: bfloat16 [4096, 12288], P('dp', 'tp'), parts along dimension 0
- up: bfloat16 [4096, 12288], P('dp', 'tp'), parts along dimension 0
- w_gate: bfloat16 [4096, 12288], P(None, 'tp')
- w_up: bfloat16 [4096, 12288], P(None, 'tp')
- w_down: bfloat16 [12288, 4096], P('tp')
Outputs:
- output 1: bfloat16 [4096, 4096], P('dp'), parts along dimension 0
- output 2: bfloat16 [8192, 12288], P('dp', 'tp'), parts along dimension 0
- output 3: bfloat16 [8192, 12288], P('dp', 'tp'), parts along dimension 0
- output 4: bfloat16 [24576, 4096], P(('dp', 'tp')), parts along dimension 0
There are 2 independent parts. A program takes and returns all parts, laid end to end along the dimension named above; an argument that names none is the same for every part.
All inputs are finite; a program needn't handle non-finite values.
Results may differ from a plain program's by a relative error of at most 0.012.
Values are sent between devices in bfloat16 or wider.
A program may use at most 2 GiB of HBM per device.

v0:
```python
import jax
import jax.numpy as jnp
from jax import lax
from jax.sharding import PartitionSpec as P


def act(gate, up):
    return jax.nn.silu(gate) * up


def solution(mesh):
    def step(x, dy, gate, up, w_gate, w_up, w_down):
        hidden, back = jax.vjp(act, gate.astype(jnp.float32), up.astype(jnp.float32))
        d_hidden = jnp.dot(dy, w_down.T, preferred_element_type=jnp.float32)
        d_gate, d_up = (g.astype(jnp.bfloat16) for g in back(d_hidden))
        term = jnp.dot(d_gate, w_gate.T, preferred_element_type=jnp.float32) + jnp.dot(d_up, w_up.T, preferred_element_type=jnp.float32)
        dx = lax.psum(term.astype(jnp.bfloat16), "tp")
        dw_gate = jnp.dot(x.T, d_gate, preferred_element_type=jnp.float32)
        dw_up = jnp.dot(x.T, d_up, preferred_element_type=jnp.float32)
        dw_down = jnp.dot(hidden.astype(jnp.bfloat16).T, dy, preferred_element_type=jnp.float32)
        return dx, *(g.astype(jnp.bfloat16) for g in (dw_gate, dw_up, dw_down))

    tokens, columns, rows = P("dp", None), P(None, "tp"), P("tp", None)
    return jax.shard_map(
        step,
        mesh=mesh,
        in_specs=(tokens, tokens, P("dp", "tp"), P("dp", "tp"), columns, columns, rows),
        out_specs=(tokens, P("dp", "tp"), P("dp", "tp"), P(("dp", "tp"), None)),
        check_vma=False,
    )
```

profile of v0, /device:TPU:0, one launch (start us, length us, event | category | flops | bytes accessed | tf_op | source)
XLA Modules:
  0.0 401.1 jit_solution(8724858323400050045)
XLA Ops:
  7.2 0.0 all-reduce.2.cloned.1.call-start
  7.2 23.6 %fusion.6 = (bf16[2048,768]{1,0:T(8,128)(2,1)}, f32[2048,768]{1,0:T(8,128)}) fusion(bf16[2048,768]{1,0:T(8,128)(2,1)} %param.9, bf16[2048,768]{1,0:T(8,128)(2,1)} %param.10, bf16[2048,4096]{1,0:T(8,128)(2,1)} %param.8, bf16[768,4096]{1,0:T(8,128)(2,1)} %param.13), kind=kOutput, calls=%fused_computation.16 | convolution fusion | flops 12905349120 | bytes 38797312 | tf_op jit(solution)/shard_map/dot_general | solution.py:14
  30.8 0.0 copy-start
  30.8 22.3 %fusion.11 = f32[2048,4096]{1,0:T(8,128)} fusion(bf16[2048,768]{1,0:T(8,128)(2,1)} %get-tuple-element.8, bf16[4096,768]{1,0:T(8,128)(2,1)} %param.11), kind=kOutput, calls=%fused_computation.21 | convolution fusion | flops 12884901888 | bytes 42991616 | tf_op jit(solution)/shard_map/dot_general | solution.py:16
  53.1 0.0 copy-done
  53.1 26.2 %add_convert_fusion = bf16[2048,4096]{1,0:T(8,128)(2,1)} fusion(f32[2048,4096]{1,0:T(8,128)} %fusion.11, bf16[4096,768]{1,0:T(8,128)(2,1)} %param.12, f32[2048,768]{1,0:T(8,128)} %get-tuple-element.9, bf16[2048,768]{1,0:T(8,128)(2,1)S(1)} %copy-done), kind=kOutput, calls=%fused_computation | convolution fusion | flops 12912689152 | bytes 66060288 | tf_op jit(solution)/shard_map/dot_general | solution.py:16
  79.3 0.0 all-reduce.2.cloned.1.call-update
  79.3 19.5 %fusion.7 = bf16[4096,768]{0,1:T(8,128)(2,1)} fusion(bf16[2048,768]{1,0:T(8,128)(2,1)} %get-tuple-element.8, bf16[2048,4096]{1,0:T(8,128)(2,1)} %param.7), kind=kOutput, calls=%fused_computation.18 | convolution fusion | flops 12888047616 | bytes 26214400 | tf_op jit(solution)/shard_map/dot_general | solution.py:18
  98.8 8.6 %copy.11 = bf16[4096,768]{1,0:T(8,128)(2,1)} copy(bf16[4096,768]{0,1:T(8,128)(2,1)} %fusion.7) | data formatting | bytes 12582912
  107.4 21.2 %fusion.8 = bf16[4096,768]{0,1:T(8,128)(2,1)} fusion(bf16[2048,4096]{1,0:T(8,128)(2,1)} %param.7, f32[2048,768]{1,0:T(8,128)} %get-tuple-element.9, bf16[2048,768]{1,0:T(8,128)(2,1)S(1)} %copy-done), kind=kOutput, calls=%fused_computation.19 | convolution fusion | flops 12899057664 | bytes 32505856 | tf_op jit(solution)/shard_map/dot_general | solution.py:19
  128.6 8.6 %copy.12 = bf16[4096,768]{1,0:T(8,128)(2,1)} copy(bf16[4096,768]{0,1:T(8,128)(2,1)} %fusion.8) | data formatting | bytes 12582912
  137.2 21.2 %convolution_convert_fusion = bf16[768,4096]{1,0:T(8,128)(2,1)} fusion(bf16[2048,4096]{1,0:T(8,128)(2,1)} %param.8, bf16[2048,768]{1,0:T(8,128)(2,1)} %param.10, bf16[2048,768]{1,0:T(8,128)(2,1)S(1)} %copy-done), kind=kOutput, calls=%fused_computation.7 | convolution fusion | flops 12900630528 | bytes 29360128 | tf_op jit(solution)/shard_map/dot_general | solution.py:20
  158.4 221.8 %all-reduce.2.cloned.1.call-done = bf16[2048,4096]{1,0:T(8,128)(2,1)} async-done(((bf16[2048,4096]{1,0:T(8,128)(2,1)}), bf16[2048,4096]{1,0:T(8,128)(2,1)}) %all-reduce.2.cloned.1.call-update) | async-done | bytes 16777232 | tf_op jit(solution)/shard_map/psum | solution.py:17
  380.2 14.1 %copy.14 = bf16[2048,4096]{1,0:T(8,128)(2,1)} copy(bf16[2048,4096]{1,0:T(8,128)(2,1)} %all-reduce.2.cloned.1.call-done) | data formatting | bytes 33554432
Async XLA Ops:
  7.2 373.0 %all-reduce.2.cloned.1.call-start = ((), (), s32[]{:S(2)}) async-start(), calls=%async_computation | async-start | bytes 33554432 | tf_op jit(solution)/shard_map/psum | solution.py:17
  30.8 22.3 %copy-start = (bf16[2048,768]{1,0:T(8,128)(2,1)S(1)}, bf16[2048,768]{1,0:T(8,128)(2,1)}, u32[]{:S(2)}) copy-start(bf16[2048,768]{1,0:T(8,128)(2,1)} %param.9) | copy-start | bytes 9437188
Sparse Core Ops, SparseCore 0:
  79.4 300.7 all-reduce.1
where the time goes:
time: 402 us; the launch traced here: 401 us
  waiting for transfers between devices  222 us (55%)
  matrix products  134 us (33%)
  local copies, waits for them, and re-layouts  31.3 us (8%)
  between operations  14 us (3%)
    psum x1, waiting for transfers between devices, step(): dx = lax.psum(term.astype(jnp.bfloat16), 'tp')  222 us
    unnamed x5, local copies, waits for them, and re-layouts  31.3 us
    dot_general x1, matrix products, step(): jnp.dot(d_up, w_up.T, preferred_element_type=jnp.float32)  26.2 us
    dot_general x1, matrix products, step(): d_hidden = jnp.dot(dy, w_down.T, preferred_element_type=jnp.float32)  23.6 us
    dot_general x1, matrix products, step(): jnp.dot(d_gate, w_gate.T, preferred_element_type=jnp.float32)  22.3 us
    dot_general x1, matrix products, step(): dw_up = jnp.dot(x.T, d_up, preferred_element_type=jnp.float32)  21.2 us
    dot_general x1, matrix products, step(): jnp.dot(hidden.astype(jnp.bfloat16).T, dy, preferred_element_type=jnp.flo...  21.2 us
    dot_general x1, matrix products, step(): dw_gate = jnp.dot(x.T, d_gate, preferred_element_type=jnp.float32)  19.5 us
  transfers between devices with their start and end apart: 1, of which 1 were waited for; matrix products, arithmetic and copies ran while one was open for 20% of the time, Pallas kernels for 0%

commit v1 on v0

v1 whole, which is shorter than its diff:
```python
import jax
import jax.numpy as jnp
from jax import lax
from jax.experimental import pallas as pl
from jax.experimental.pallas import tpu as pltpu
from jax.sharding import PartitionSpec as P

F32, BF16 = jnp.float32, jnp.bfloat16
ROWS, D, F = 2048, 4096, 768
BR = 512
BC = 512
NG = 2048 // BC
N = (ROWS // BR) * NG
H = BC // 2
OFF = (0, 1, 3, 5, 7, 9, 11, 13, 15, 17)
NA = OFF[5] + 1
DW0 = 17
TW = 256
NW = D // TW
T = max(N + OFF[9], DW0 + NW)
DEPTH = 4
NT = (((1,), (1,)), ((), ()))
TN = (((0,), (0,)), ((), ()))


def mm(a, b, dims):
    return lax.dot_general(a, b, dims, preferred_element_type=F32)


def ds(start, size):
    return pl.ds(pl.multiple_of(start, size), size)


class Chan:
    def __init__(self, cond, src, dst, send, recv=None, dev=None, depth=DEPTH):
        self.cond, self.src, self.dst, self.send, self.recv, self.dev, self.depth = cond, src, dst, send, recv, dev, depth

    def desc(self, k):
        sem = self.send.at[lax.rem(k, self.depth)]
        if self.dev is None:
            return pltpu.make_async_copy(self.src(k), self.dst(k), sem)
        return pltpu.make_async_remote_copy(
            self.src(k), self.dst(k), sem, self.recv(k), device_id=self.dev, device_id_type=pl.DeviceIdType.MESH
        )

    def _wait(self, k):
        if self.dev is None:
            self.desc(k).wait()
        else:
            self.desc(k).wait_send()

    def ready(self, k):
        @pl.when(k >= self.depth)
        def _():
            self._wait(k - self.depth)

    def start(self, k):
        self.desc(k).start()

    def go(self, k):
        self.ready(k)
        self.start(k)

    def drain(self, n):
        def run():
            @pl.loop(n - self.depth, n)
            def _(k):
                self._wait(k)

        if self.cond is None:
            run()
        else:
            pl.when(self.cond)(run)


def kernel(x, dy, gate, up, wg_h, wu_h, wd_h, out, dwg, dwu, dwd,
           wd, wg, wu, dgu, hT, dyb, gb, ub, d2d_st, d2d_rv, tmp, accA, accB,
           yA_rv, zA_rv, zB_rv, yB_rv, yA_st, zA_st, zB_st, yB_st, fA_st, fB_st, o_gu, o_d,
           ld, tl, ss, rs, d2d_r, credit):
    tp = lax.axis_index("tp")
    y, z, c = tp // 8, lax.rem(tp // 2, 4), lax.rem(tp, 2)

    def dev(yy, zz, cc):
        return {"tp": yy * 8 + zz * 2 + cc}

    pair, ynb = dev(y, z, 1 - c), dev(1 - y, z, c)
    rt, lf = dev(y, jnp.minimum(z + 1, 3), c), dev(y, jnp.maximum(z - 1, 0), c)
    z0, z1, z2, z3 = z == 0, z == 1, z == 2, z == 3
    end = jnp.logical_or(z0, z3)

    def row(k):
        return (k // NG) * BR

    def col(k, cc):
        return cc * 2048 + lax.rem(k, NG) * BC

    names_s = ["d2d", "yA", "zAR", "zAL", "zBR", "zBL", "yB", "fAl", "fAy", "fAz", "fBl", "fBy", "fBz",
               "gAR", "gAL", "gAyR", "gAyL", "gBy", "gBR", "gBL", "gp"]
    S = {n: ss.at[i] for i, n in enumerate(names_s)}
    names_r = ["yA", "zAR", "zAL", "zBR", "zBL", "yB", "gAR", "gAL", "gAyR", "gAyL", "gBy", "gBR0", "gBR1", "gBL0", "gBL1", "gp"]
    R = {n: (lambda k, i=i: rs.at[i, k]) for i, n in enumerate(names_r)}

    def oA(k, yy, rl, cc=c):
        return out.at[ds(row(k) + yy * 256 + rl * 128, 128), ds(col(k, cc), H)]

    def oB(k, rl, yy):
        return out.at[ds(row(k) + rl * 256 + yy * 128, 128), ds(col(k, c) + H, H)]

    def oB2(k, rl):
        return out.at[ds(row(k) + rl * 256, 256), ds(col(k, c) + H, H)]

    def st(ref):
        return lambda k: ref.at[lax.rem(k, DEPTH)]

    def rv(ref):
        return lambda k: ref.at[k]

    d2d = Chan(None, lambda k: d2d_st.at[lax.rem(k, 2)], lambda k: d2d_rv.at[lax.rem(k, 4)], S["d2d"],
               lambda k: d2d_r.at[lax.rem(k, 4)], pair, 2)
    yA = Chan(None, st(yA_st), rv(yA_rv), S["yA"], R["yA"], ynb)
    zA = [Chan(z < 3, st(zA_st.at[0]), rv(zA_rv.at[0]), S["zAR"], R["zAR"], rt),
          Chan(z > 0, st(zA_st.at[1]), rv(zA_rv.at[1]), S["zAL"], R["zAL"], lf)]
    zB = [Chan(z < 3, st(zB_st.at[0]), rv(zB_rv.at[0]), S["zBR"], R["zBR"], rt),
          Chan(z > 0, st(zB_st.at[1]), rv(zB_rv.at[1]), S["zBL"], R["zBL"], lf)]
    yB = Chan(end, st(yB_st), rv(yB_rv), S["yB"], R["yB"], ynb)
    fA, fB, gA, gAy, gB = [], [], [], [], []
    for rl, (fin, back, recvs) in enumerate(((z3, lf, ("gAR", "gAyR")), (z0, rt, ("gAL", "gAyL")))):
        o = lambda k, rl=rl: oA(k, y, rl)
        fA.append([Chan(fin, st(fA_st), o, S["fAl"]),
                   Chan(fin, st(fA_st), o, S["fAy"], R[recvs[1]], ynb),
                   Chan(fin, st(fA_st), o, S["fAz"], R[recvs[0]], back)])
        mid = jnp.logical_or(z1, z2)
        gA.append(Chan(mid, o, o, S["gAR" if rl == 0 else "gAL"], R[recvs[0]], back))
        nf = (z < 3) if rl == 0 else (z > 0)
        gAy.append(Chan(nf, o, o, S["gAyR" if rl == 0 else "gAyL"], R[recvs[1]], ynb))
        ob = lambda k, rl=rl: oB(k, rl, y)
        ob_other = lambda k, rl=rl: oB(k, rl, 1 - y)
        nm = "gBR" if rl == 0 else "gBL"
        by_y = lambda me, nm=nm: (lambda k: rs.at[names_r.index(nm + "0") + me, k])
        fB.append([Chan(fin, st(fB_st), ob, S["fBl"]),
                   Chan(fin, st(fB_st), ob, S["fBy"], R["gBy"], ynb),
                   Chan(fin, st(fB_st), ob, S["fBz"], by_y(y), back),
                   Chan(fin, ob_other, ob_other, S["gBy"], by_y(1 - y), back)])
        ob2 = lambda k, rl=rl: oB2(k, rl)
        gB.append(Chan(mid, ob2, ob2, S[nm], R[nm + "0"], back))
    whole = lambda k: out.at[ds(row(k), BR), ds(col(k, c), BC)]
    gp = Chan(None, whole, whole, S["gp"], R["gp"], pair)

    def got(dst, sem):
        pltpu.make_async_copy(dst, dst, sem).wait()

    pltpu.make_async_copy(wd_h, wd, ld.at[0]).start()

    def blk(b):
        r = ds(b * BR, BR)
        return [pltpu.make_async_copy(dy.at[r], dyb, ld.at[3]),
                pltpu.make_async_copy(gate.at[r], gb, ld.at[4]),
                pltpu.make_async_copy(up.at[r], ub, ld.at[5])]

    for cp in blk(0):
        cp.start()
    pltpu.make_async_copy(wg_h, wg, ld.at[1]).start()
    pltpu.make_async_copy(wu_h, wu, ld.at[2]).start()
    pltpu.make_async_copy(wd_h, wd, ld.at[0]).wait()

    def tile(j):
        s = lax.rem(j, 2)
        return [pltpu.make_async_copy(x.at[:, ds(j * TW, TW)], wg.at[ds(s * 2048, 2048), pl.ds(0, TW)], tl.at[0, s]),
                pltpu.make_async_copy(dy.at[:, ds(j * TW, TW)], wg.at[ds(s * 2048, 2048), pl.ds(TW, TW)], tl.at[1, s])]

    def tile_out(j):
        s = lax.rem(j, 2)
        return [pltpu.make_async_copy(o_gu.at[s, :, pl.ds(0, F)], dwg.at[ds(j * TW, TW)], tl.at[2, s]),
                pltpu.make_async_copy(o_gu.at[s, :, pl.ds(F, F)], dwu.at[ds(j * TW, TW)], tl.at[3, s]),
                pltpu.make_async_copy(o_d.at[s], dwd.at[:, ds(j * TW, TW)], tl.at[4, s])]

    def hidden_block(b):
        for cp in blk(b):
            cp.wait()
        r = ds(b * BR, BR)

        @pl.loop(0, F // 256)
        def _(n):
            f = ds(n * 256, 256)
            dh = mm(dyb[...], wd[f, :], NT)
            g, u = gb[:, f].astype(F32), ub[:, f].astype(F32)
            sig = jax.nn.sigmoid(g)
            silu = g * sig
            hT[f, r] = (silu * u).T.astype(BF16)
            dgu[r, f] = (dh * u * (sig + silu * (1.0 - sig))).astype(BF16)
            dgu[r, ds(F + n * 256, 256)] = (dh * silu).astype(BF16)

        @pl.when(b + 1 < ROWS // BR)
        def _():
            for cp in blk(b + 1):
                cp.start()

    def term(k, cols):
        r = ds(row(k), BR)
        return mm(dgu[r, pl.ds(0, F)], wg[cols, :], NT) + mm(dgu[r, pl.ds(F, F)], wu[cols, :], NT)

    def a0(k):
        @pl.when(lax.rem(k, NG) == 0)
        def _():
            hidden_block(k // NG)

        @pl.when(k == 0)
        def _():
            pltpu.make_async_copy(wg_h, wg, ld.at[1]).wait()
            pltpu.make_async_copy(wu_h, wu, ld.at[2]).wait()

        d2d.ready(k)
        for h in range(2):
            d2d_st[lax.rem(k, 2), :, pl.ds(h * H, H)] = term(k, ds(col(k, 1 - c) + h * H, H)).astype(BF16)

        @pl.when(k >= 4)
        def _():
            pl.semaphore_wait(credit, 1)

        d2d.start(k)

    def a1(k):
        s, q = lax.rem(k, NA), lax.rem(k, DEPTH)
        s4 = lax.rem(k, 4)
        got(d2d_rv.at[s4], d2d_r.at[s4])
        yA.ready(k)
        tmp[...] = term(k, ds(col(k, c), H)) + d2d_rv[s4, :, pl.ds(0, H)].astype(F32)
        yA_st[q] = tmp[ds((1 - y) * 256, 256), :].astype(BF16)
        yA.start(k)
        accA[s] = tmp[ds(y * 256, 256), :]
        accB[s] = term(k, ds(col(k, c) + H, H)) + d2d_rv[s4, :, pl.ds(H, H)].astype(F32)

        @pl.when(k < N - 4)
        def _():
            pl.semaphore_signal(credit, 1, device_id=pair, device_id_type=pl.DeviceIdType.MESH)

        for rl, first in ((0, z0), (1, z3)):
            @pl.when(first)
            def _():
                zB[rl].ready(k)
                zB_st[rl, q] = accB[s, pl.ds(rl * 256, 256), :].astype(BF16)
                zB[rl].start(k)

    def passA(k, rl):
        s, q = lax.rem(k, NA), lax.rem(k, DEPTH)
        got(zA_rv.at[rl, k], R["zAR" if rl == 0 else "zAL"](k))
        zA[rl].ready(k)
        zA_st[rl, q] = (accA[s, pl.ds(rl * 128, 128), :] + zA_rv[rl, k].astype(F32)).astype(BF16)
        zA[rl].start(k)

    def passB(k, rl):
        s, q = lax.rem(k, NA), lax.rem(k, DEPTH)
        got(zB_rv.at[rl, k], R["zBR" if rl == 0 else "zBL"](k))
        zB[rl].ready(k)
        zB_st[rl, q] = (accB[s, pl.ds(rl * 256, 256), :] + zB_rv[rl, k].astype(F32)).astype(BF16)
        zB[rl].start(k)

    def a2(k):
        s, q = lax.rem(k, NA), lax.rem(k, DEPTH)
        pl.when(z1)(lambda: passB(k, 0))
        pl.when(z2)(lambda: passB(k, 1))
        got(yA_rv.at[k], R["yA"](k))
        accA[s] = accA[s] + yA_rv[k].astype(F32)
        for rl, first in ((0, z0), (1, z3)):
            @pl.when(first)
            def _():
                zA[rl].ready(k)
                zA_st[rl, q] = accA[s, pl.ds(rl * 128, 128), :].astype(BF16)
                zA[rl].start(k)

    def a3(k):
        pl.when(z2)(lambda: passB(k, 0))
        pl.when(z1)(lambda: passB(k, 1))
        pl.when(z1)(lambda: passA(k, 0))
        pl.when(z2)(lambda: passA(k, 1))

    def a4(k):
        s, q = lax.rem(k, NA), lax.rem(k, DEPTH)
        for rl, fin in ((0, z3), (1, z0)):
            @pl.when(fin)
            def _():
                got(zB_rv.at[rl, k], R["zBR" if rl == 0 else "zBL"](k))
                yB.ready(k)
                r = pl.ds(rl * 256, 256)
                accB[s, r, :] = accB[s, r, :] + zB_rv[rl, k].astype(F32)
                yB_st[q] = accB[s, ds(rl * 256 + (1 - y) * 128, 128), :].astype(BF16)
                yB.start(k)
        pl.when(z2)(lambda: passA(k, 0))
        pl.when(z1)(lambda: passA(k, 1))

    def a5(k):
        s, q = lax.rem(k, NA), lax.rem(k, DEPTH)
        for rl, fin in ((0, z3), (1, z0)):
            @pl.when(fin)
            def _():
                got(yB_rv.at[k], R["yB"](k))
                for ch in fB[rl][:3]:
                    ch.ready(k)
                fB_st[q] = (accB[s, ds(rl * 256 + y * 128, 128), :] + yB_rv[k].astype(F32)).astype(BF16)
                for ch in fB[rl][:3]:
                    ch.start(k)
                got(zA_rv.at[rl, k], R["zAR" if rl == 0 else "zAL"](k))
                for ch in fA[rl]:
                    ch.ready(k)
                fA_st[q] = (accA[s, pl.ds(rl * 128, 128), :] + zA_rv[rl, k].astype(F32)).astype(BF16)
                for ch in fA[rl]:
                    ch.start(k)

    def fwdA(k, rl, z_too):
        got(oA(k, y, rl), R["gAR" if rl == 0 else "gAL"](k))
        if z_too:
            gA[rl].go(k)
        gAy[rl].go(k)

    def a6(k):
        pl.when(z2)(lambda: fwdA(k, 0, True))
        pl.when(z1)(lambda: fwdA(k, 1, True))
        for rl, fin in ((0, z3), (1, z0)):
            @pl.when(fin)
            def _():
                fA[rl][0].desc(k).wait()
                fB[rl][0].desc(k).wait()
                got(oB(k, rl, 1 - y), R["gBy"](k))
                fB[rl][3].go(k)

    def a7(k):
        pl.when(z1)(lambda: fwdA(k, 0, True))
        pl.when(z2)(lambda: fwdA(k, 1, True))
        for rl, m in ((0, z2), (1, z1)):
            @pl.when(m)
            def _():
                nm = "gBR" if rl == 0 else "gBL"
                for yy in range(2):
                    got(oB(k, rl, yy), R[nm + str(yy)](k))
                gB[rl].go(k)

    def a8(k):
        pl.when(z0)(lambda: fwdA(k, 0, False))
        pl.when(z3)(lambda: fwdA(k, 1, False))
        for rl, m in ((0, z1), (1, z2)):
            @pl.when(m)
            def _():
                got(oB2(k, rl), R["gBR0" if rl == 0 else "gBL0"](k))
                gB[rl].go(k)

    def a9(k):
        for rl, m in enumerate((z0, z3)):
            @pl.when(m)
            def _():
                got(oB2(k, rl), R["gBR0" if rl == 0 else "gBL0"](k))
            got(oA(k, 1 - y, rl), R["gAyR" if rl == 0 else "gAyL"](k))
        gp.go(k)

    for rl in range(2):
        for ch in (fA[rl][0], fB[rl][0]):
            ch.ready = lambda k: None

    def weights(j):
        for cp in tile(j):
            cp.wait()

        @pl.when(j + 1 < NW)
        def _():
            for cp in tile(j + 1):
                cp.start()

        @pl.when(j >= 2)
        def _():
            for cp in tile_out(j - 2):
                cp.wait()

        s = lax.rem(j, 2)
        o_gu[s] = mm(wg[ds(s * 2048, 2048), pl.ds(0, TW)], dgu[...], TN).astype(BF16)
        o_d[s] = mm(hT[...], wg[ds(s * 2048, 2048), pl.ds(TW, TW)], (((1,), (0,)), ((), ()))).astype(BF16)
        for cp in tile_out(j):
            cp.start()

    stages = (a0, a1, a2, a3, a4, a5, a6, a7, a8, a9)

    @pl.loop(0, T)
    def _(t):
        for i in reversed(range(10)):
            k = t - OFF[i]

            @pl.when(jnp.logical_and(k >= 0, k < N))
            def _():
                stages[i](k)

        @pl.when(t == DW0 - 1)
        def _():
            for cp in tile(0):
                cp.start()

        j = t - DW0

        @pl.when(jnp.logical_and(j >= 0, j < NW))
        def _():
            weights(j)

    for j in (NW - 2, NW - 1):
        for cp in tile_out(j):
            cp.wait()
    d2d.drain(N)
    yA.drain(N)
    for ch in (*zA, *zB, yB, *fA[0][1:], *fA[1][1:], *fB[0][1:], *fB[1][1:], *gA, *gAy, *gB, gp):
        ch.drain(N)

    @pl.loop(0, N)
    def _(k):
        got(out.at[ds(row(k), BR), ds(col(k, 1 - c), BC)], R["gp"](k))


def solution(mesh):
    def step(x, dy, gate, up, w_gate, w_up, w_down):
        hbm = pl.BlockSpec(memory_space=pl.ANY)
        V, DMA = pltpu.VMEM, pltpu.SemaphoreType.DMA
        return pl.pallas_call(
            kernel,
            name="mlp_bwd",
            out_shape=[
                jax.ShapeDtypeStruct((ROWS, D), BF16),
                jax.ShapeDtypeStruct((D, F), BF16),
                jax.ShapeDtypeStruct((D, F), BF16),
                jax.ShapeDtypeStruct((F, D), BF16),
            ],
            in_specs=[hbm] * 7,
            out_specs=[hbm] * 4,
            scratch_shapes=[
                V((F, D), BF16), V((D, F), BF16), V((D, F), BF16),
                V((ROWS, 2 * F), BF16), V((F, ROWS), BF16),
                V((BR, D), BF16), V((BR, F), BF16), V((BR, F), BF16),
                V((2, BR, BC), BF16), V((4, BR, BC), BF16),
                V((BR, H), F32), V((NA, 256, H), F32), V((NA, 512, H), F32),
                V((N, 256, H), BF16), V((2, N, 128, H), BF16), V((2, N, 256, H), BF16), V((N, 128, H), BF16),
                V((DEPTH, 256, H), BF16), V((2, DEPTH, 128, H), BF16), V((2, DEPTH, 256, H), BF16), V((DEPTH, 128, H), BF16),
                V((DEPTH, 128, H), BF16), V((DEPTH, 128, H), BF16),
                V((2, TW, 2 * F), BF16), V((2, F, TW), BF16),
                DMA((6,)), DMA((5, 2)), DMA((21, DEPTH)), DMA((16, N)), DMA((4,)),
                pltpu.SemaphoreType.REGULAR,
            ],
            compiler_params=pltpu.CompilerParams(has_side_effects=True, vmem_limit_bytes=67043328),
            cost_estimate=pl.CostEstimate(flops=77_000_000_000, bytes_accessed=100_000_000, transcendentals=0),
        )(x, dy, gate, up, w_gate, w_up, w_down)

    tokens, columns, rows = P("dp", None), P(None, "tp"), P("tp", None)
    return jax.shard_map(
        step,
        mesh=mesh,
        in_specs=(tokens, tokens, P("dp", "tp"), P("dp", "tp"), columns, columns, rows),
        out_specs=(tokens, P("dp", "tp"), P("dp", "tp"), P(("dp", "tp"), None)),
        check_vma=False,
    )
```

time: 402 us -> 229 us (0.57)
  waiting for transfers between devices: 222 us -> 0 us
  Pallas kernels: 0 us -> 202 us
  matrix products: 134 us -> 0 us
  between operations: 14 us -> 0.66 us
  local copies, waits for them, and re-layouts: 31.3 us -> 26.4 us
    psum x1 -> x0, waiting for transfers between devices: 222 us -> none  [step(): dx = lax.psum(term.astype(jnp.bfloat16), 'tp')]
    pallas_call x0 -> x1, Pallas kernels: none -> 202 us  [step(): pl.pallas_call(kernel, name='mlp_bwd', out_shape=[jax.ShapeDtypeStruct((R...]
    dot_general x6 -> x0, matrix products: 134 us -> none  [the longest x1 26.2 us: step(): jnp.dot(d_up, w_up.T, preferred_element_type=jnp.float32)]
    unnamed x5 -> x12, local copies, waits for them, and re-layouts: 31.3 us -> 26.4 us
  transfers between devices with their start and end apart: 1 -> 0, of which waited for: 1 -> 0; matrix products, arithmetic and copies ran while one was open for 20% -> 0% of each run, Pallas kernels for 0% -> 0%
where the time goes in v1:
time: 229 us
  Pallas kernels  202 us (88%)
  local copies, waits for them, and re-layouts  26.4 us (12%)
    pallas_call x1, Pallas kernels, step(): pl.pallas_call(kernel, name='mlp_bwd', out_shape=[jax.ShapeDtypeStruct((R...  202 us
    unnamed x12, local copies, waits for them, and re-layouts  26.4 us

profile of v1, /device:TPU:0, one launch (start us, length us, event | category | flops | bytes accessed | tf_op | source)
XLA Modules:
  0.0 229.0 jit_solution(10839638792945306873)
XLA Ops:
  0.6 201.9 %mlp_bwd.1 = (bf16[2048,4096]{1,0:T(8,128)(2,1)}, bf16[4096,768]{1,0:T(8,128)(2,1)}, bf16[4096,768]{1,0:T(8,128)(2,1)}, bf16[768,4096]{1,0:T(8,128)(2,1)}) custom-call(bf16[2048,4096]{1,0:T(8,128)(2,1)} %x.1, bf16[2048,4096]{1,0:T(8,128)(2,1)} %dy.1, bf16[2048,768]{1,0:T(8,128)(2,1)} %gate.1, bf16[2048,768]{1,0:T(8,128)(2,1)} %up.1, bf16[4096,768]{1,0:T(8,128)(2,1)} %wg_h.1, ...), custom_call_target="tpu_custom_call" | custom-call | flops 76999999488 | bytes 100000000 | tf_op jit(solution)/shard_map/mlp_bwd/pallas_call | solution.py:417
  202.6 0.0 copy-start.1
  202.6 14.6 %copy.15 = bf16[2048,4096]{1,0:T(8,128)(2,1)} copy(bf16[2048,4096]{1,0:T(8,128)(2,1)} %get-tuple-element.8) | data formatting | bytes 33554432
  217.1 0.0 copy-done.1
  217.1 0.0 copy-start
  217.1 0.0 slice-start
  217.2 3.2 %copy.16 = bf16[4096,768]{1,0:T(8,128)(2,1)} copy(bf16[4096,768]{1,0:T(8,128)(2,1)S(1)} %copy-done.1) | data formatting | bytes 12582912
  220.3 1.9 copy-done
  222.2 0.0 slice-start.1
  222.2 3.1 %copy.17 = bf16[4096,768]{1,0:T(8,128)(2,1)} copy(bf16[4096,768]{1,0:T(8,128)(2,1)S(1)} %copy-done) | data formatting | bytes 12582912
  225.3 0.0 slice-done
  225.3 1.0 slice-done.1
  226.3 2.7 %copy.18 = bf16[768,4096]{1,0:T(8,128)(2,1)} copy(bf16[768,4096]{1,0:T(8,128)(2,1)S(1)} %bitcast.1) | data formatting | bytes 12582912
  (1 shorter events, 0.0 us)
Async XLA Ops:
  202.6 14.6 %copy-start.1 = (bf16[4096,768]{1,0:T(8,128)(2,1)S(1)}, bf16[4096,768]{1,0:T(8,128)(2,1)}, u32[]{:S(2)}) copy-start(bf16[4096,768]{1,0:T(8,128)(2,1)} %get-tuple-element.9) | copy-start | bytes 18874372
  217.1 5.1 %copy-start = (bf16[4096,768]{1,0:T(8,128)(2,1)S(1)}, bf16[4096,768]{1,0:T(8,128)(2,1)}, u32[]{:S(2)}) copy-start(bf16[4096,768]{1,0:T(8,128)(2,1)} %get-tuple-element.10) | copy-start | bytes 18874372
  217.1 8.1 %slice-start = ((s8[6291456]{0:T(1024)(128)(4,1)}), s8[4194304]{0:T(1024)(128)(4,1)S(1)}, s32[]{:S(2)}) async-start(s8[6291456]{0:T(1024)(128)(4,1)} %bitcast), calls=%async_computation | async-start | bytes 8388608
  222.2 4.1 %slice-start.1 = ((s8[6291456]{0:T(1024)(128)(4,1)}), s8[2097152]{0:T(1024)(128)(4,1)S(1)}, s32[]{:S(2)}) async-start(s8[6291456]{0:T(1024)(128)(4,1)} %bitcast), calls=%async_computation.1 | async-start | bytes 4194304

commit v2 on v0

v2 whole, which is shorter than its diff:
```python
import functools

import jax
import jax.numpy as jnp
from jax import lax
from jax.experimental import pallas as pl
from jax.experimental.pallas import tpu as pltpu
from jax.sharding import PartitionSpec as P

F32, BF16 = jnp.float32, jnp.bfloat16
ROWS, D, F = 2048, 4096, 768
BR = 512
H = 256
NG = 2048 // H
N = (ROWS // BR) * NG
PAT = "ABABA"
PP = len(PAT)
CH = {r: [k for k in range(N) if PAT[k % PP] == r] for r in "AB"}
CNT = {r: len(CH[r]) for r in "AB"}
OFF = {"A": (0, 2, 7, 7, 10, 16, 17, 19, 31, 38), "B": (0, 2, 3, 5, 15, 20, 24, 26, 30, 38)}
ORDER = (9, 10, 2, 6, 4, 5, 8, 1, 3, 0, 7)
HS = (0, 5, 15, 20)
DW0 = 25
TW = 256
NW = D // TW
UP = PP - PP % 2
TT = max(-(-(N + OFF["A"][9]) // PP), DW0 // PP + 2 * NW // UP)


def turn(r, i, stage):
    return CH[r][i] + OFF[r][stage], ORDER.index(stage)


def slots(r):
    return next(n for n in range(1, CNT[r]) if all(turn(r, i + n, 1) > turn(r, i, 5) for i in range(CNT[r] - n)))


NS = {r: slots(r) for r in "AB"}
DEPTH = 4
DR = 8
NT = (((1,), (1,)), ((), ()))
TN = (((0,), (0,)), ((), ()))
NN = (((1,), (0,)), ((), ()))


def mm(a, b, dims):
    return lax.dot_general(a, b, dims, preferred_element_type=F32)


def ds(start, size):
    return pl.ds(pl.multiple_of(start, size), size)


class Chan:
    def __init__(self, n, cond, src, dst, send, recv=None, dev=None):
        self.n, self.cond, self.src, self.dst, self.send, self.recv, self.dev = n, cond, src, dst, send, recv, dev

    def desc(self, k, i):
        sem = self.send.at[lax.rem(i, DEPTH)]
        if self.dev is None:
            return pltpu.make_async_copy(self.src(k, i), self.dst(k, i), sem)
        return pltpu.make_async_remote_copy(
            self.src(k, i), self.dst(k, i), sem, self.recv(i), device_id=self.dev, device_id_type=pl.DeviceIdType.MESH
        )

    def wait(self, k, i):
        if self.dev is None:
            self.desc(k, i).wait()
        else:
            self.desc(k, i).wait_send()

    def ready(self, k, i):
        @pl.when(i >= DEPTH)
        def _():
            self.wait(k, i)

    def start(self, k, i):
        self.desc(k, i).start()

    def go(self, k, i):
        self.ready(k, i)
        self.start(k, i)

    def drain(self):
        def run():
            @pl.loop(self.n - DEPTH, self.n)
            def _(i):
                self.wait(0, i)

        if self.cond is None:
            run()
        else:
            pl.when(self.cond)(run)


def kernel(x, dy, gate, up, wg_h, wu_h, wd_h, out, dwg, dwu, dwd,
           wd, wg, wu, dgu, hT, xb, gb, ub, d2d_st, d2d_rv, tmp, accA, accB,
           yA_rv, zA_rv, zB_rv, yB_rv, yA_st, zA_st, zB_st, yB_st, fA_st, fB_st, o_gu, o_d,
           ld, tl, ss, rs, credit):
    tp = lax.axis_index("tp")
    y, z, c = tp // 8, lax.rem(tp // 2, 4), lax.rem(tp, 2)

    def dev(yy, zz, cc):
        return {"tp": yy * 8 + zz * 2 + cc}

    pair, ynb = dev(y, z, 1 - c), dev(1 - y, z, c)
    rt, lf = dev(y, jnp.minimum(z + 1, 3), c), dev(y, jnp.maximum(z - 1, 0), c)
    z0, z1, z2, z3 = z == 0, z == 1, z == 2, z == 3
    mid = jnp.logical_or(z1, z2)
    end = jnp.logical_or(z0, z3)
    nA, nB = CNT["A"], CNT["B"]

    def row(k):
        return (k // NG) * BR

    def col(k, cc):
        return cc * 2048 + lax.rem(k, NG) * H

    names_s = ["d2d", "yA", "zAR", "zAL", "zBR", "zBL", "yB", "fAl", "fAy", "fAz", "fBl", "fBy", "fBz",
               "gAR", "gAL", "gAyR", "gAyL", "gBy", "gBR", "gBL", "gp"]
    S = {n: ss.at[i] for i, n in enumerate(names_s)}
    names_r = ["yA", "zAR", "zAL", "zBR", "zBL", "yB", "gAR", "gAL", "gAyR", "gAyL", "gBy",
               "gBR0", "gBR1", "gBL0", "gBL1", "gp", "d2d"]
    R = {n: (lambda i, j=j: rs.at[j, i]) for j, n in enumerate(names_r)}

    def oA(k, yy, rl):
        return out.at[ds(row(k) + yy * 256 + rl * 128, 128), ds(col(k, c), H)]

    def oB(k, rl, yy):
        return out.at[ds(row(k) + rl * 256 + yy * 128, 128), ds(col(k, c), H)]

    def oB2(k, rl):
        return out.at[ds(row(k) + rl * 256, 256), ds(col(k, c), H)]

    def st(ref):
        return lambda k, i: ref.at[lax.rem(i, DEPTH)]

    def rv(ref):
        return lambda k, i: ref.at[i]

    d2d = Chan(N, None, st(d2d_st), lambda k, i: d2d_rv.at[lax.rem(i, DR)], S["d2d"],
               lambda i: R["d2d"](lax.rem(i, DR)), pair)
    yA = Chan(nA, None, st(yA_st), rv(yA_rv), S["yA"], R["yA"], ynb)
    zA = [Chan(nA, z < 3, st(zA_st.at[0]), rv(zA_rv.at[0]), S["zAR"], R["zAR"], rt),
          Chan(nA, z > 0, st(zA_st.at[1]), rv(zA_rv.at[1]), S["zAL"], R["zAL"], lf)]
    zB = [Chan(nB, z < 3, st(zB_st.at[0]), rv(zB_rv.at[0]), S["zBR"], R["zBR"], rt),
          Chan(nB, z > 0, st(zB_st.at[1]), rv(zB_rv.at[1]), S["zBL"], R["zBL"], lf)]
    yB = Chan(nB, end, st(yB_st), rv(yB_rv), S["yB"], R["yB"], ynb)
    fA, fB, gA, gAy, gB, loc = [], [], [], [], [], []
    for rl, (fin, back, recvs) in enumerate(((z3, lf, ("gAR", "gAyR")), (z0, rt, ("gAL", "gAyL")))):
        o = lambda k, i, rl=rl: oA(k, y, rl)
        fA.append([Chan(nA, fin, st(fA_st), o, S["fAy"], R[recvs[1]], ynb),
                   Chan(nA, fin, st(fA_st), o, S["fAz"], R[recvs[0]], back)])
        gA.append(Chan(nA, mid, o, o, S["gAR" if rl == 0 else "gAL"], R[recvs[0]], back))
        nf = (z < 3) if rl == 0 else (z > 0)
        gAy.append(Chan(nA, nf, o, o, S["gAyR" if rl == 0 else "gAyL"], R[recvs[1]], ynb))
        ob = lambda k, i, rl=rl: oB(k, rl, y)
        ob_other = lambda k, i, rl=rl: oB(k, rl, 1 - y)
        nm = "gBR" if rl == 0 else "gBL"
        by_y = lambda me, nm=nm: (lambda i: rs.at[names_r.index(nm + "0") + me, i])
        fB.append([Chan(nB, fin, st(fB_st), ob, S["fBy"], R["gBy"], ynb),
                   Chan(nB, fin, st(fB_st), ob, S["fBz"], by_y(y), back),
                   Chan(nB, fin, ob_other, ob_other, S["gBy"], by_y(1 - y), back)])
        ob2 = lambda k, i, rl=rl: oB2(k, rl)
        gB.append(Chan(nB, mid, ob2, ob2, S[nm], R[nm + "0"], back))
        loc.append((Chan(nA, fin, st(fA_st), o, S["fAl"]), Chan(nB, fin, st(fB_st), ob, S["fBl"])))
    whole = lambda k, i: out.at[ds(row(k), BR), ds(col(k, c), H)]
    gp = Chan(N, None, whole, whole, S["gp"], R["gp"], pair)

    def got(dst, sem):
        pltpu.make_async_copy(dst, dst, sem).wait()

    def dy_block(b):
        r = ds(b * BR, BR)
        cps = [pltpu.make_async_copy(dy.at[r, pl.ds(p * 256, 256)], xb.at[p // 4, pl.ds((p % 4) * 512, 512)], ld.at[3])
               for p in range(16)]
        return cps + [pltpu.make_async_copy(gate.at[r], gb, ld.at[4]), pltpu.make_async_copy(up.at[r], ub, ld.at[5])]

    def wd_part(n):
        return pltpu.make_async_copy(wd_h.at[ds(n * 256, 256)], wd.at[ds(n * 256, 256)], ld.at[6 + n])

    wd_part(0).start()
    for cp in dy_block(0):
        cp.start()
    wd_part(1).start()
    wd_part(2).start()
    pltpu.make_async_copy(wg_h, wg, ld.at[1]).start()
    pltpu.make_async_copy(wu_h, wu, ld.at[2]).start()

    def tile(kind, j):
        s = lax.rem(j, 2)
        return pltpu.make_async_copy((x, dy)[kind].at[:, ds(j * TW, TW)], xb.at[2 * kind + s], tl.at[kind, s])

    def tile_out(kind, j):
        s = lax.rem(j, 2)
        if kind == 0:
            return [pltpu.make_async_copy(o_gu.at[s, :, pl.ds(0, F)], dwg.at[ds(j * TW, TW)], tl.at[2, s]),
                    pltpu.make_async_copy(o_gu.at[s, :, pl.ds(F, F)], dwu.at[ds(j * TW, TW)], tl.at[3, s])]
        return [pltpu.make_async_copy(o_d.at[s], dwd.at[:, ds(j * TW, TW)], tl.at[4, s])]

    def hidden_block(b):
        got(xb, ld.at[3])
        got(gb, ld.at[4])
        got(ub, ld.at[5])
        r = ds(b * BR, BR)

        @pl.loop(0, F // 256)
        def _(n):
            pl.when(b == 0)(lambda: wd_part(n).wait())
            f = ds(n * 256, 256)
            dh = sum(mm(xb[p // 4, pl.ds((p % 4) * 512, 512), :], wd[f, pl.ds(p * 256, 256)], NT) for p in range(16))
            g, u = gb[:, f].astype(F32), ub[:, f].astype(F32)
            sig = jax.nn.sigmoid(g)
            silu = g * sig
            hT[f, r] = (silu * u).T.astype(BF16)
            dgu[r, f] = (dh * u * (sig + silu * (1.0 - sig))).astype(BF16)
            dgu[r, ds(F + n * 256, 256)] = (dh * silu).astype(BF16)

        @pl.when(b + 1 < ROWS // BR)
        def _():
            for cp in dy_block(b + 1):
                cp.start()

        @pl.when(b + 1 == ROWS // BR)
        def _():
            tile(0, 0).start()
            tile(1, 0).start()

    def term(k, cols):
        r = ds(row(k), BR)
        return mm(dgu[r, pl.ds(0, F)], wg[cols, :], NT) + mm(dgu[r, pl.ds(F, F)], wu[cols, :], NT)

    def a0(k, i, cls):
        @pl.when(k == 0)
        def _():
            pltpu.make_async_copy(wg_h, wg, ld.at[1]).wait()
            pltpu.make_async_copy(wu_h, wu, ld.at[2]).wait()

        d2d.ready(k, k)
        d2d_st[lax.rem(k, DEPTH)] = term(k, ds(col(k, 1 - c), H)).astype(BF16)

        @pl.when(k >= DR)
        def _():
            pl.semaphore_wait(credit, 1)

        d2d.start(k, k)

    def a1(k, i, cls):
        s, q, s8 = lax.rem(i, NS[cls]), lax.rem(i, DEPTH), lax.rem(k, DR)
        got(d2d_rv.at[s8], R["d2d"](s8))
        if cls == "A":
            yA.ready(k, i)
            tmp[...] = term(k, ds(col(k, c), H)) + d2d_rv[s8].astype(F32)
            yA_st[q] = tmp[ds((1 - y) * 256, 256), :].astype(BF16)
            yA.start(k, i)
            accA[s] = tmp[ds(y * 256, 256), :]
        else:
            accB[s] = term(k, ds(col(k, c), H)) + d2d_rv[s8].astype(F32)
            for rl, first in ((0, z0), (1, z3)):
                @pl.when(first)
                def _():
                    zB[rl].ready(k, i)
                    zB_st[rl, q] = accB[s, pl.ds(rl * 256, 256), :].astype(BF16)
                    zB[rl].start(k, i)

        @pl.when(k < N - DR)
        def _():
            pl.semaphore_signal(credit, 1, device_id=pair, device_id_type=pl.DeviceIdType.MESH)

    def passA(k, i, rl):
        s, q = lax.rem(i, NS["A"]), lax.rem(i, DEPTH)
        got(zA_rv.at[rl, i], R["zAR" if rl == 0 else "zAL"](i))
        zA[rl].ready(k, i)
        zA_st[rl, q] = (accA[s, pl.ds(rl * 128, 128), :] + zA_rv[rl, i].astype(F32)).astype(BF16)
        zA[rl].start(k, i)

    def passB(k, i, rl):
        s, q = lax.rem(i, NS["B"]), lax.rem(i, DEPTH)
        got(zB_rv.at[rl, i], R["zBR" if rl == 0 else "zBL"](i))
        zB[rl].ready(k, i)
        zB_st[rl, q] = (accB[s, pl.ds(rl * 256, 256), :] + zB_rv[rl, i].astype(F32)).astype(BF16)
        zB[rl].start(k, i)

    def a2(k, i, cls):
        s, q = lax.rem(i, NS[cls]), lax.rem(i, DEPTH)
        if cls == "B":
            pl.when(z1)(lambda: passB(k, i, 0))
            pl.when(z2)(lambda: passB(k, i, 1))
            return
        got(yA_rv.at[i], R["yA"](i))
        accA[s] = accA[s] + yA_rv[i].astype(F32)
        for rl, first in ((0, z0), (1, z3)):
            @pl.when(first)
            def _():
                zA[rl].ready(k, i)
                zA_st[rl, q] = accA[s, pl.ds(rl * 128, 128), :].astype(BF16)
                zA[rl].start(k, i)

    def a3(k, i, cls):
        if cls == "B":
            pl.when(z2)(lambda: passB(k, i, 0))
            pl.when(z1)(lambda: passB(k, i, 1))
        else:
            pl.when(z1)(lambda: passA(k, i, 0))
            pl.when(z2)(lambda: passA(k, i, 1))

    def a4(k, i, cls):
        s, q = lax.rem(i, NS[cls]), lax.rem(i, DEPTH)
        if cls == "A":
            pl.when(z2)(lambda: passA(k, i, 0))
            pl.when(z1)(lambda: passA(k, i, 1))
            return
        for rl, fin in ((0, z3), (1, z0)):
            @pl.when(fin)
            def _():
                got(zB_rv.at[rl, i], R["zBR" if rl == 0 else "zBL"](i))
                yB.ready(k, i)
                r = pl.ds(rl * 256, 256)
                accB[s, r, :] = accB[s, r, :] + zB_rv[rl, i].astype(F32)
                yB_st[q] = accB[s, ds(rl * 256 + (1 - y) * 128, 128), :].astype(BF16)
                yB.start(k, i)

    def a5(k, i, cls):
        s, q = lax.rem(i, NS[cls]), lax.rem(i, DEPTH)
        for rl, fin in ((0, z3), (1, z0)):
            @pl.when(fin)
            def _():
                if cls == "B":
                    got(yB_rv.at[i], R["yB"](i))
                    for ch in fB[rl][:2]:
                        ch.ready(k, i)
                    fB_st[q] = (accB[s, ds(rl * 256 + y * 128, 128), :] + yB_rv[i].astype(F32)).astype(BF16)
                    for ch in (*fB[rl][:2], loc[rl][1]):
                        ch.start(k, i)
                else:
                    got(zA_rv.at[rl, i], R["zAR" if rl == 0 else "zAL"](i))
                    for ch in fA[rl]:
                        ch.ready(k, i)
                    fA_st[q] = (accA[s, pl.ds(rl * 128, 128), :] + zA_rv[rl, i].astype(F32)).astype(BF16)
                    for ch in (*fA[rl], loc[rl][0]):
                        ch.start(k, i)

    def fwdA(k, i, rl, z_too):
        got(oA(k, y, rl), R["gAR" if rl == 0 else "gAL"](i))
        if z_too:
            gA[rl].go(k, i)
        gAy[rl].go(k, i)

    def a6(k, i, cls):
        if cls == "A":
            pl.when(z2)(lambda: fwdA(k, i, 0, True))
            pl.when(z1)(lambda: fwdA(k, i, 1, True))
            return
        for rl, fin in ((0, z3), (1, z0)):
            @pl.when(fin)
            def _():
                got(oB(k, rl, 1 - y), R["gBy"](i))
                fB[rl][2].go(k, i)

    def a7(k, i, cls):
        if cls == "A":
            pl.when(z1)(lambda: fwdA(k, i, 0, True))
            pl.when(z2)(lambda: fwdA(k, i, 1, True))
            return
        for rl, m in ((0, z2), (1, z1)):
            @pl.when(m)
            def _():
                nm = "gBR" if rl == 0 else "gBL"
                for yy in range(2):
                    got(oB(k, rl, yy), R[nm + str(yy)](i))
                gB[rl].go(k, i)

    def a8(k, i, cls):
        if cls == "A":
            pl.when(z0)(lambda: fwdA(k, i, 0, False))
            pl.when(z3)(lambda: fwdA(k, i, 1, False))
            return
        for rl, m in ((0, z1), (1, z2)):
            @pl.when(m)
            def _():
                got(oB2(k, rl), R["gBR0" if rl == 0 else "gBL0"](i))
                gB[rl].go(k, i)

    def a9(k, i, cls):
        for rl, m in enumerate((z0, z3)):
            if cls == "B":
                @pl.when(m)
                def _():
                    got(oB2(k, rl), R["gBR0" if rl == 0 else "gBL0"](i))
            else:
                got(oA(k, 1 - y, rl), R["gAyR" if rl == 0 else "gAyL"](i))
        gp.go(k, k)

    def weights(kind, j):
        tile(kind, j).wait()

        @pl.when(j + 1 < NW)
        def _():
            tile(kind, j + 1).start()

        @pl.when(j >= 2)
        def _():
            for cp in tile_out(kind, j - 2):
                cp.wait()

        s = lax.rem(j, 2)
        if kind == 0:
            o_gu[s] = mm(xb[s], dgu[...], TN).astype(BF16)
        else:
            o_d[s] = mm(hT[...], xb[2 + s], NN).astype(BF16)
        for cp in tile_out(kind, j):
            cp.start()

    stages = (a0, a1, a2, a3, a4, a5, a6, a7, a8, a9)

    def settle(k, i, cls):
        for rl, fin in ((0, z3), (1, z0)):
            pl.when(fin)(lambda: loc[rl]["AB".index(cls)].wait(k, i))

    @pl.loop(0, TT)
    def _(tt):
        for par in range(PP):
            t = tt * PP + par

            def chunk(cls, stage, run):
                ph = (par - OFF[cls][stage]) % PP
                if PAT[ph] != cls:
                    return
                rnd = tt + (par - OFF[cls][stage] - ph) // PP
                k, i = rnd * PP + ph, rnd * PAT.count(cls) + PAT[:ph].count(cls)

                @pl.when(jnp.logical_and(k >= 0, k < N))
                def _():
                    run(k, i, cls)

            if par == 0:
                b = sum((t >= s).astype(jnp.int32) for s in HS[1:])
                pl.when(functools.reduce(jnp.logical_or, [t == s for s in HS]))(lambda: hidden_block(b))
            for stage in ORDER:
                if stage == 0:
                    pl.when(t < N)(lambda: a0(t, t, None))
                elif stage == 10:
                    j = (tt - DW0 // PP) * (UP // 2) + par // 2

                    if par < UP:
                        @pl.when(jnp.logical_and(tt >= DW0 // PP, j < NW))
                        def _():
                            weights(par % 2, j)
                else:
                    for cls in "AB":
                        chunk(cls, stage, stages[stage])
            for cls in "AB":
                chunk(cls, 5, settle)

    for kind in range(2):
        for j in (NW - 2, NW - 1):
            for cp in tile_out(kind, j):
                cp.wait()
    for ch in (d2d, yA, *zA, *zB, yB, *fA[0], *fA[1], *fB[0], *fB[1], *gA, *gAy, *gB, gp):
        ch.drain()

    @pl.loop(0, N)
    def _(k):
        got(out.at[ds(row(k), BR), ds(col(k, 1 - c), H)], R["gp"](k))


def solution(mesh):
    def step(x, dy, gate, up, w_gate, w_up, w_down):
        hbm = pl.BlockSpec(memory_space=pl.ANY)
        V, DMA = pltpu.VMEM, pltpu.SemaphoreType.DMA
        return pl.pallas_call(
            kernel,
            name="mlp_bwd",
            out_shape=[
                jax.ShapeDtypeStruct((ROWS, D), BF16),
                jax.ShapeDtypeStruct((D, F), BF16),
                jax.ShapeDtypeStruct((D, F), BF16),
                jax.ShapeDtypeStruct((F, D), BF16),
            ],
            in_specs=[hbm] * 7,
            out_specs=[hbm] * 4,
            scratch_shapes=[
                V((F, D), BF16), V((D, F), BF16), V((D, F), BF16),
                V((ROWS, 2 * F), BF16), V((F, ROWS), BF16),
                V((4, ROWS, TW), BF16), V((BR, F), BF16), V((BR, F), BF16),
                V((DEPTH, BR, H), BF16), V((DR, BR, H), BF16),
                V((BR, H), F32), V((NS["A"], 256, H), F32), V((NS["B"], 512, H), F32),
                V((CNT["A"], 256, H), BF16), V((2, CNT["A"], 128, H), BF16),
                V((2, CNT["B"], 256, H), BF16), V((CNT["B"], 128, H), BF16),
                V((DEPTH, 256, H), BF16), V((2, DEPTH, 128, H), BF16), V((2, DEPTH, 256, H), BF16), V((DEPTH, 128, H), BF16),
                V((DEPTH, 128, H), BF16), V((DEPTH, 128, H), BF16),
                V((2, TW, 2 * F), BF16), V((2, F, TW), BF16),
                DMA((9,)), DMA((5, 2)), DMA((21, DEPTH)), DMA((17, N)),
                pltpu.SemaphoreType.REGULAR,
            ],
            compiler_params=pltpu.CompilerParams(has_side_effects=True, vmem_limit_bytes=67043328),
            cost_estimate=pl.CostEstimate(flops=77_000_000_000, bytes_accessed=100_000_000, transcendentals=0),
        )(x, dy, gate, up, w_gate, w_up, w_down)

    tokens, columns, rows = P("dp", None), P(None, "tp"), P("tp", None)
    return jax.shard_map(
        step,
        mesh=mesh,
        in_specs=(tokens, tokens, P("dp", "tp"), P("dp", "tp"), columns, columns, rows),
        out_specs=(tokens, P("dp", "tp"), P("dp", "tp"), P(("dp", "tp"), None)),
        check_vma=False,
    )
```

time: 402 us -> 209 us (0.52)
  waiting for transfers between devices: 222 us -> 0 us
  Pallas kernels: 0 us -> 181 us
  matrix products: 134 us -> 0 us
  between operations: 14 us -> 0.66 us
  local copies, waits for them, and re-layouts: 31.3 us -> 26.4 us
    psum x1 -> x0, waiting for transfers between devices: 222 us -> none  [step(): dx = lax.psum(term.astype(jnp.bfloat16), 'tp')]
    pallas_call x0 -> x1, Pallas kernels: none -> 181 us  [step(): pl.pallas_call(kernel, name='mlp_bwd', out_shape=[jax.ShapeDtypeStruct((R...]
    dot_general x6 -> x0, matrix products: 134 us -> none  [the longest x1 26.2 us: step(): jnp.dot(d_up, w_up.T, preferred_element_type=jnp.float32)]
    unnamed x5 -> x12, local copies, waits for them, and re-layouts: 31.3 us -> 26.4 us
  transfers between devices with their start and end apart: 1 -> 0, of which waited for: 1 -> 0; matrix products, arithmetic and copies ran while one was open for 20% -> 0% of each run, Pallas kernels for 0% -> 0%
where the time goes in v2:
time: 209 us; the launch traced here: 208 us
  Pallas kernels  181 us (87%)
  local copies, waits for them, and re-layouts  26.4 us (13%)
    pallas_call x1, Pallas kernels, step(): pl.pallas_call(kernel, name='mlp_bwd', out_shape=[jax.ShapeDtypeStruct((R...  181 us
    unnamed x12, local copies, waits for them, and re-layouts  26.4 us

profile of v2, /device:TPU:0, one launch (start us, length us, event | category | flops | bytes accessed | tf_op | source)
XLA Modules:
  0.0 208.5 jit_solution(14544132644979308702)
XLA Ops:
  0.6 181.4 %mlp_bwd.1 = (bf16[2048,4096]{1,0:T(8,128)(2,1)}, bf16[4096,768]{1,0:T(8,128)(2,1)}, bf16[4096,768]{1,0:T(8,128)(2,1)}, bf16[768,4096]{1,0:T(8,128)(2,1)}) custom-call(bf16[2048,4096]{1,0:T(8,128)(2,1)} %x.1, bf16[2048,4096]{1,0:T(8,128)(2,1)} %dy.1, bf16[2048,768]{1,0:T(8,128)(2,1)} %gate.1, bf16[2048,768]{1,0:T(8,128)(2,1)} %up.1, bf16[4096,768]{1,0:T(8,128)(2,1)} %wg_h.1, ...), custom_call_target="tpu_custom_call" | custom-call | flops 76999999488 | bytes 100000000 | tf_op jit(solution)/shard_map/mlp_bwd/pallas_call | solution.py:471
  182.0 0.0 copy-start.1
  182.1 14.6 %copy.15 = bf16[2048,4096]{1,0:T(8,128)(2,1)} copy(bf16[2048,4096]{1,0:T(8,128)(2,1)} %get-tuple-element.8) | data formatting | bytes 33554432
  196.6 0.0 copy-done.1
  196.6 0.0 copy-start
  196.6 0.0 slice-start
  196.6 3.2 %copy.16 = bf16[4096,768]{1,0:T(8,128)(2,1)} copy(bf16[4096,768]{1,0:T(8,128)(2,1)S(1)} %copy-done.1) | data formatting | bytes 12582912
  199.8 1.9 copy-done
  201.7 0.0 slice-start.1
  201.7 3.1 %copy.17 = bf16[4096,768]{1,0:T(8,128)(2,1)} copy(bf16[4096,768]{1,0:T(8,128)(2,1)S(1)} %copy-done) | data formatting | bytes 12582912
  204.8 0.0 slice-done
  204.8 1.0 slice-done.1
  205.8 2.7 %copy.18 = bf16[768,4096]{1,0:T(8,128)(2,1)} copy(bf16[768,4096]{1,0:T(8,128)(2,1)S(1)} %bitcast.1) | data formatting | bytes 12582912
  (1 shorter events, 0.0 us)
Async XLA Ops:
  182.0 14.6 %copy-start.1 = (bf16[4096,768]{1,0:T(8,128)(2,1)S(1)}, bf16[4096,768]{1,0:T(8,128)(2,1)}, u32[]{:S(2)}) copy-start(bf16[4096,768]{1,0:T(8,128)(2,1)} %get-tuple-element.9) | copy-start | bytes 18874372
  196.6 5.1 %copy-start = (bf16[4096,768]{1,0:T(8,128)(2,1)S(1)}, bf16[4096,768]{1,0:T(8,128)(2,1)}, u32[]{:S(2)}) copy-start(bf16[4096,768]{1,0:T(8,128)(2,1)} %get-tuple-element.10) | copy-start | bytes 18874372
  196.6 8.1 %slice-start = ((s8[6291456]{0:T(1024)(128)(4,1)}), s8[4194304]{0:T(1024)(128)(4,1)S(1)}, s32[]{:S(2)}) async-start(s8[6291456]{0:T(1024)(128)(4,1)} %bitcast), calls=%async_computation | async-start | bytes 8388608
  201.7 4.1 %slice-start.1 = ((s8[6291456]{0:T(1024)(128)(4,1)}), s8[2097152]{0:T(1024)(128)(4,1)S(1)}, s32[]{:S(2)}) async-start(s8[6291456]{0:T(1024)(128)(4,1)} %bitcast), calls=%async_computation.1 | async-start | bytes 4194304

commit v3 on v2

--- a/solution.py
+++ b/solution.py
@@ -13,12 +13,12 @@
 H = 256
 NG = 2048 // H
 N = (ROWS // BR) * NG
-PAT = "ABABA"
+PAT = "AABAB"
 PP = len(PAT)
 CH = {r: [k for k in range(N) if PAT[k % PP] == r] for r in "AB"}
 CNT = {r: len(CH[r]) for r in "AB"}
-OFF = {"A": (0, 2, 7, 7, 10, 16, 17, 19, 31, 38), "B": (0, 2, 3, 5, 15, 20, 24, 26, 30, 38)}
-ORDER = (9, 10, 2, 6, 4, 5, 8, 1, 3, 0, 7)
+OFF = {"A": (0, 2, 7, 7, 10, 15, 17, 19, 31, 38), "B": (0, 2, 3, 5, 15, 20, 24, 26, 30, 38)}
+ORDER = (10, 9, 2, 6, 4, 5, 8, 1, 3, 0, 7)
 HS = (0, 5, 15, 20)
 DW0 = 25
 TW = 256
@@ -38,6 +38,8 @@
 NS = {r: slots(r) for r in "AB"}
 DEPTH = 4
 DR = 8
+WR, SR = 256, 1024
+CR, CL = 8, 4
 NT = (((1,), (1,)), ((), ()))
 TN = (((0,), (0,)), ((), ()))
 NN = (((1,), (0,)), ((), ()))
@@ -464,11 +466,41 @@
         got(out.at[ds(row(k), BR), ds(col(k, 1 - c), H)], R["gp"](k))
 
 
+def copy_kernel(*refs):
+    ins, outs, (wide, slim, si, so) = refs[:4], refs[4:8], refs[8:]
+    parts = []
+    for a, b in zip(ins, outs):
+        rows, cols = a.shape
+        n = WR if cols == D else SR
+        parts += [(a.at[pl.ds(r, n)], b.at[pl.ds(r, n)], wide if cols == D else slim) for r in range(0, rows, n)]
+
+    def take(q):
+        a, _, buf = parts[q]
+        return pltpu.make_async_copy(a, buf.at[q % CR], si.at[q % CR])
+
+    def give(q):
+        _, b, buf = parts[q]
+        return pltpu.make_async_copy(buf.at[q % CR], b, so.at[q % CR])
+
+    for q in range(CR - CL):
+        take(q).start()
+    for q in range(len(parts)):
+        take(q).wait()
+        give(q).start()
+        nxt = q + CR - CL
+        if nxt < len(parts):
+            if nxt >= CR:
+                give(nxt - CR).wait()
+            take(nxt).start()
+    for q in range(len(parts) - CR, len(parts)):
+        give(q).wait()
+
+
 def solution(mesh):
     def step(x, dy, gate, up, w_gate, w_up, w_down):
         hbm = pl.BlockSpec(memory_space=pl.ANY)
         V, DMA = pltpu.VMEM, pltpu.SemaphoreType.DMA
-        return pl.pallas_call(
+        held = pl.pallas_call(
             kernel,
             name="mlp_bwd",
             out_shape=[
@@ -496,6 +528,15 @@
             compiler_params=pltpu.CompilerParams(has_side_effects=True, vmem_limit_bytes=67043328),
             cost_estimate=pl.CostEstimate(flops=77_000_000_000, bytes_accessed=100_000_000, transcendentals=0),
         )(x, dy, gate, up, w_gate, w_up, w_down)
+        return pl.pallas_call(
+            copy_kernel,
+            name="results",
+            out_shape=[jax.ShapeDtypeStruct(a.shape, a.dtype) for a in held],
+            in_specs=[hbm] * 4,
+            out_specs=[hbm] * 4,
+            scratch_shapes=[V((CR, WR, D), BF16), V((CR, SR, F), BF16), DMA((CR,)), DMA((CR,))],
+            compiler_params=pltpu.CompilerParams(vmem_limit_bytes=67043328),
+        )(*held)
 
     tokens, columns, rows = P("dp", None), P(None, "tp"), P("tp", None)
     return jax.shard_map(

time: 209 us -> 207 us (level)
  local copies, waits for them, and re-layouts: 26.4 us -> 0 us
  Pallas kernels: 181 us -> 206 us
    unnamed x12 -> x0, local copies, waits for them, and re-layouts: 26.4 us -> none
    pallas_call x0 -> x1, Pallas kernels: none -> 24 us  [step(): pl.pallas_call(copy_kernel, name='results', out_shape=[jax.ShapeDtypeStru...]
where the time goes in v3:
time: 207 us
  Pallas kernels  206 us (100%)
    pallas_call x1, Pallas kernels, step(): pl.pallas_call(kernel, name='mlp_bwd', out_shape=[jax.ShapeDtypeStruct((R...  182 us
    pallas_call x1, Pallas kernels, step(): pl.pallas_call(copy_kernel, name='results', out_shape=[jax.ShapeDtypeStru...  24 us

profile of v3, /device:TPU:0, one launch (start us, length us, event | category | flops | bytes accessed | tf_op | source)
XLA Modules:
  0.0 206.6 jit_solution(14367363383742662119)
XLA Ops:
  0.6 182.0 %mlp_bwd.1 = (bf16[2048,4096]{1,0:T(8,128)(2,1)}, bf16[4096,768]{1,0:T(8,128)(2,1)}, bf16[4096,768]{1,0:T(8,128)(2,1)}, bf16[768,4096]{1,0:T(8,128)(2,1)}) custom-call(bf16[2048,4096]{1,0:T(8,128)(2,1)} %x.1, bf16[2048,4096]{1,0:T(8,128)(2,1)} %dy.1, bf16[2048,768]{1,0:T(8,128)(2,1)} %gate.1, bf16[2048,768]{1,0:T(8,128)(2,1)} %up.1, bf16[4096,768]{1,0:T(8,128)(2,1)} %wg_h.1, ...), custom_call_target="tpu_custom_call" | custom-call | flops 76999999488 | bytes 100000000 | tf_op jit(solution)/shard_map/mlp_bwd/pallas_call | solution.py:503
  182.6 24.0 %results.1 = (bf16[2048,4096]{1,0:T(8,128)(2,1)}, bf16[4096,768]{1,0:T(8,128)(2,1)}, bf16[4096,768]{1,0:T(8,128)(2,1)}, bf16[768,4096]{1,0:T(8,128)(2,1)}) custom-call(bf16[2048,4096]{1,0:T(8,128)(2,1)} %get-tuple-element.8.refs_0_, bf16[4096,768]{1,0:T(8,128)(2,1)} %get-tuple-element.9.refs_1_, bf16[4096,768]{1,0:T(8,128)(2,1)} %get-tuple-element.10.refs_2_, ...), custom_call_target="tpu_custom_call" | custom-call | tf_op jit(solution)/shard_map/results/pallas_call | solution.py:531

commit v4 on v3

--- a/solution.py
+++ b/solution.py
@@ -38,8 +38,8 @@
 NS = {r: slots(r) for r in "AB"}
 DEPTH = 4
 DR = 8
-WR, SR = 256, 1024
-CR, CL = 8, 4
+WR, SR = 128, 512
+CR, CL = 16, 8
 NT = (((1,), (1,)), ((), ()))
 TN = (((0,), (0,)), ((), ()))
 NN = (((1,), (0,)), ((), ()))
@@ -178,6 +178,16 @@
                for p in range(16)]
         return cps + [pltpu.make_async_copy(gate.at[r], gb, ld.at[4]), pltpu.make_async_copy(up.at[r], ub, ld.at[5])]
 
+    barrier = pltpu.get_barrier_semaphore()
+    for cond, d in ((None, pair), (None, ynb), (z < 3, rt), (z > 0, lf)):
+        def hello(d=d):
+            pl.semaphore_signal(barrier, 1, device_id=d, device_id_type=pl.DeviceIdType.MESH)
+
+        if cond is None:
+            hello()
+        else:
+            pl.when(cond)(hello)
+
     def wd_part(n):
         return pltpu.make_async_copy(wd_h.at[ds(n * 256, 256)], wd.at[ds(n * 256, 256)], ld.at[6 + n])
 
@@ -188,6 +198,8 @@
     wd_part(2).start()
     pltpu.make_async_copy(wg_h, wg, ld.at[1]).start()
     pltpu.make_async_copy(wu_h, wu, ld.at[2]).start()
+
+    pl.semaphore_wait(barrier, jnp.where(end, 3, 4))
 
     def tile(kind, j):
         s = lax.rem(j, 2)
@@ -525,7 +537,7 @@
                 DMA((9,)), DMA((5, 2)), DMA((21, DEPTH)), DMA((17, N)),
                 pltpu.SemaphoreType.REGULAR,
             ],
-            compiler_params=pltpu.CompilerParams(has_side_effects=True, vmem_limit_bytes=67043328),
+            compiler_params=pltpu.CompilerParams(collective_id=0, has_side_effects=True, vmem_limit_bytes=67043328),
             cost_estimate=pl.CostEstimate(flops=77_000_000_000, bytes_accessed=100_000_000, transcendentals=0),
         )(x, dy, gate, up, w_gate, w_up, w_down)
         return pl.pallas_call(

time: 207 us -> 201 us (0.971)
  Pallas kernels: 206 us -> 200 us
    pallas_call x1, Pallas kernels: 182 us -> 176 us  [step(): pl.pallas_call(kernel, name='mlp_bwd', out_shape=[jax.ShapeDtypeStruct((R...]
where the time goes in v4:
time: 201 us
  Pallas kernels  200 us (100%)
    pallas_call x1, Pallas kernels, step(): pl.pallas_call(kernel, name='mlp_bwd', out_shape=[jax.ShapeDtypeStruct((R...  176 us
    pallas_call x1, Pallas kernels, step(): pl.pallas_call(copy_kernel, name='results', out_shape=[jax.ShapeDtypeStru...  24 us

profile of v4, /device:TPU:0, one launch (start us, length us, event | category | flops | bytes accessed | tf_op | source)
XLA Modules:
  0.0 201.0 jit_solution(8015845593823195142)
XLA Ops:
  0.6 176.3 %mlp_bwd.1 = (bf16[2048,4096]{1,0:T(8,128)(2,1)}, bf16[4096,768]{1,0:T(8,128)(2,1)}, bf16[4096,768]{1,0:T(8,128)(2,1)}, bf16[768,4096]{1,0:T(8,128)(2,1)}) custom-call(bf16[2048,4096]{1,0:T(8,128)(2,1)} %x.1, bf16[2048,4096]{1,0:T(8,128)(2,1)} %dy.1, bf16[2048,768]{1,0:T(8,128)(2,1)} %gate.1, bf16[2048,768]{1,0:T(8,128)(2,1)} %up.1, bf16[4096,768]{1,0:T(8,128)(2,1)} %wg_h.1, ...), custom_call_target="tpu_custom_call" | custom-call | flops 76999999488 | bytes 100000000 | tf_op jit(solution)/shard_map/mlp_bwd/pallas_call | solution.py:515
  177.0 24.0 %results.1 = (bf16[2048,4096]{1,0:T(8,128)(2,1)}, bf16[4096,768]{1,0:T(8,128)(2,1)}, bf16[4096,768]{1,0:T(8,128)(2,1)}, bf16[768,4096]{1,0:T(8,128)(2,1)}) custom-call(bf16[2048,4096]{1,0:T(8,128)(2,1)} %get-tuple-element.8.refs_0_, bf16[4096,768]{1,0:T(8,128)(2,1)} %get-tuple-element.9.refs_1_, bf16[4096,768]{1,0:T(8,128)(2,1)} %get-tuple-element.10.refs_2_, ...), custom_call_target="tpu_custom_call" | custom-call | tf_op jit(solution)/shard_map/results/pallas_call | solution.py:543
